TPU v7x, 32 devices: a whole 2x2x4 slice. The times are simulated.
32 devices in a mesh: seq: 8 (over z, y), tp: 4 (over x, core).
Axes of the slice: x: 2, y: 2, z: 4, core: 2. Of those that a mesh axis runs over, the one named last changes fastest.
Arguments:
- inputs: bfloat16 [2, 32, 8192], P(None, 'seq', 'tp'), may hold values from -6 to 6
- out_grad: bfloat16 [2, 32, 8192], P(None, 'seq', 'tp'), may hold values from -6 to 6
- gate_weight: bfloat16 [8192, 14848], P('tp', 'seq'), may hold values from -0.0625 to 0.0625
- up_weight: bfloat16 [8192, 14848], P('tp', 'seq'), may hold values from -0.0625 to 0.0625
- down_weight: bfloat16 [14848, 8192], P('seq', 'tp'), may hold values from -0.0625 to 0.0625
Outputs:
- input_grad: bfloat16 [2, 32, 8192], P(None, 'seq', 'tp')
- gate_grad: float32 [8192, 14848], P('tp', 'seq')
- up_grad: float32 [8192, 14848], P('tp', 'seq')
- down_grad: float32 [14848, 8192], P('seq', 'tp')
All inputs are finite; a program needn't handle non-finite values.
Results may differ from a plain program's by a relative error of at most 0.0049.
Values may be sent and summed in bfloat16 or wider, within the bound.
No kernel may reach another device: no remote copies, remote signals or barrier semaphores. Data moves between devices by JAX's collectives and lax.ppermute only.
A program may use at most 128 MiB of HBM per device.

v0:
```python
import jax
import jax.numpy as jnp
from jax import lax
from jax.sharding import PartitionSpec as P


def per_device(inputs, out_grad, gate_weight, up_weight, down_weight):
    blocks = inputs.shape[0]
    local_rows = inputs.shape[1]
    width_count = lax.axis_size("tp")
    block_tokens = local_rows * lax.axis_size("seq")
    share_rows = block_tokens // width_count
    share_start = lax.axis_index("tp") * share_rows
    contract_first = (((0,), (0,)), ((), ()))
    contract_last = (((1,), (1,)), ((), ()))
    totals = None
    results = [None] * blocks
    for index in range(blocks):
        whole_in = lax.all_gather(inputs[index], "seq", axis=0, tiled=True)
        whole_grad = lax.all_gather(out_grad[index], "seq", axis=0, tiled=True)
        gate_part = jnp.dot(whole_in, gate_weight, preferred_element_type=jnp.float32)
        up_part = jnp.dot(whole_in, up_weight, preferred_element_type=jnp.float32)
        gate, up_proj = lax.psum((gate_part, up_part), "tp")
        hidden_share = lax.psum_scatter(
            lax.dot_general(
                whole_grad, down_weight, contract_last, preferred_element_type=jnp.float32
            ),
            "tp",
            scatter_dimension=0,
            tiled=True,
        )
        gate_share = lax.dynamic_slice_in_dim(gate, share_start, share_rows, 0)
        up_share = lax.dynamic_slice_in_dim(up_proj, share_start, share_rows, 0)
        sig = jax.nn.sigmoid(gate_share)
        up_local = (hidden_share * gate_share * sig).astype(jnp.bfloat16)
        gate_local = (hidden_share * up_share * sig * (1.0 + gate_share * (1.0 - sig))).astype(
            jnp.bfloat16
        )
        front_unit_gate = lax.all_gather(gate_local, "tp", axis=0, tiled=True)
        front_unit_up = lax.all_gather(up_local, "tp", axis=0, tiled=True)
        hidden = (jax.nn.silu(gate) * up_proj).astype(jnp.bfloat16)
        down_term = lax.dot_general(
            hidden, whole_grad, contract_first, preferred_element_type=jnp.float32
        )
        gate_term = lax.dot_general(
            whole_in, front_unit_gate, contract_first, preferred_element_type=jnp.float32
        )
        up_term = lax.dot_general(
            whole_in, front_unit_up, contract_first, preferred_element_type=jnp.float32
        )
        terms = (gate_term, up_term, down_term)
        if totals is None:
            totals = terms
        else:
            totals = (totals[0] + terms[0], totals[1] + terms[1], totals[2] + terms[2])
        first = lax.dot_general(
            front_unit_gate, gate_weight, contract_last, preferred_element_type=jnp.float32
        )
        second = lax.dot_general(
            front_unit_up, up_weight, contract_last, preferred_element_type=jnp.float32
        )
        results[index] = lax.psum_scatter(
            first + second, "seq", scatter_dimension=0, tiled=True
        ).astype(jnp.bfloat16)
    return (jnp.stack(results), totals[0], totals[1], totals[2])


def solution(mesh):
    return jax.shard_map(
        per_device,
        mesh=mesh,
        in_specs=(
            P(None, "seq", "tp"),
            P(None, "seq", "tp"),
            P("tp", "seq"),
            P("tp", "seq"),
            P("seq", "tp"),
        ),
        out_specs=(P(None, "seq", "tp"), P("tp", "seq"), P("tp", "seq"), P("seq", "tp")),
        check_vma=False,
    )
```

profile of v0, /device:TPU:0, one launch (start us, length us, event | category | flops | bytes accessed | tf_op | source)
XLA Modules:
  0.0 335.3 jit_solution(6774601214005411477)
XLA Ops:
  8.2 32.8 %all-gather.3 = bf16[1,32,2048]{2,0,1:T(2,128)(2,1)S(1)} all-gather(bf16[1,4,2048]{2,0,1:T(2,128)(2,1)S(1)} %copy.24), channel_id=5, replica_groups=mesh['seq'=8,'tp'=4] {'seq'}, dimensions={1}, use_global_device_ids=true | all-gather | bytes 147456 | tf_op jit(solution)/shard_map/all_gather | solution.py:19
  41.1 30.7 %all-gather.1 = bf16[1,32,2048]{2,0,1:T(2,128)(2,1)S(1)} all-gather(bf16[1,4,2048]{2,0,1:T(2,128)(2,1)S(1)} %copy.22), channel_id=3, replica_groups=mesh['seq'=8,'tp'=4] {'seq'}, dimensions={1}, use_global_device_ids=true | all-gather | bytes 147456 | tf_op jit(solution)/shard_map/all_gather | solution.py:19
  71.9 6.4 %fusion.13 = f32[32,1856]{1,0:T(8,128)} fusion(bf16[2048,1856]{0,1:T(8,128)(2,1)} %param.7, bf16[1,32,2048]{2,1,0:T(8,128)(2,1)S(1)} %copy.18), kind=kOutput, calls=%fused_computation.20 | convolution fusion | flops 243269632 | bytes 7970816 | tf_op jit(solution)/shard_map/dot_general | solution.py:21
  78.3 3.0 fusion.15
  81.4 3.0 fusion.2
  84.4 3.0 fusion.4
  87.5 30.7 %all-gather.2 = bf16[1,32,2048]{2,0,1:T(2,128)(2,1)S(1)} all-gather(bf16[1,4,2048]{2,0,1:T(2,128)(2,1)S(1)} %copy.23), channel_id=4, replica_groups=mesh['seq'=8,'tp'=4] {'seq'}, dimensions={1}, use_global_device_ids=true | all-gather | bytes 147456 | tf_op jit(solution)/shard_map/all_gather | solution.py:20
  118.3 32.9 %all-gather = bf16[1,32,2048]{2,0,1:T(2,128)(2,1)} all-gather(bf16[1,4,2048]{2,0,1:T(2,128)(2,1)S(1)} %copy.21), channel_id=2, replica_groups=mesh['seq'=8,'tp'=4] {'seq'}, dimensions={1}, use_global_device_ids=true | all-gather | bytes 147456 | tf_op jit(solution)/shard_map/all_gather | solution.py:20
  151.2 4.0 %fusion.19 = f32[32,1856]{1,0:T(8,128)} fusion(bf16[1856,2048]{1,0:T(8,128)(2,1)S(1)} %bitcast.63, bf16[1,32,2048]{2,0,1:T(2,128)(2,1)} %all-gather), kind=kOutput, calls=%fused_computation.26 | convolution fusion | flops 243269632 | bytes 7970816 | tf_op jit(solution)/shard_map/dot_general | solution.py:25
  155.2 3.0 fusion.7
  160.8 40.2 %all-reduce.9.cloned.1.call-done = (f32[32,1856]{1,0:T(8,128)}, f32[32,1856]{1,0:T(8,128)}, f32[32,1856]{1,0:T(8,128)}, f32[32,1856]{1,0:T(8,128)}, f32[32,1856]{1,0:T(8,128)}, /*index=5*/f32[32,1856]{1,0:T(8,128)}) async-done(((f32[32,1856]{1,0:T(8,128)}, f32[32,1856]{1,0:T(8,128)}, f32[32,1856]{1,0:T(8,128)}, f32[32,1856]{1,0:T(8,128)}, f32[32,1856]{1,0:T(8,128)}, /*index=5*/f32[32,1856]{1,0:T(8,128)}), ...) | async-done | bytes 1425424 | tf_op jit(solution)/shard_map/psum | solution.py:23
  201.0 3.5 %fusion.17 = f32[1856,2048]{1,0:T(8,128)S(1)} fusion(f32[32,1856]{1,0:T(8,128)} %get-tuple-element.9, f32[32,1856]{1,0:T(8,128)} %get-tuple-element.11, bf16[1,32,2048]{2,0,1:T(2,128)(2,1)} %all-gather), kind=kOutput, calls=%fused_computation.24 | convolution fusion | flops 243625984 | bytes 15810560 | tf_op jit(solution)/shard_map/dot_general | solution.py:42
  205.5 5.4 %all_gather.26 = bf16[32,1856]{1,0:T(8,128)(2,1)S(1)} all-gather(bf16[8,1856]{1,0:T(8,128)(2,1)S(1)} %get-tuple-element.13), channel_id=1, replica_groups=mesh['seq'=8,'tp'=4] {'tp'}, dimensions={0}, use_global_device_ids=true | all-gather | bytes 148480 | tf_op jit(solution)/shard_map/all_gather | solution.py:39
  212.3 7.8 %fusion.11 = f32[1856,2048]{1,0:T(8,128)} fusion(bf16[32,1856]{1,0:T(8,128)(2,1)S(1)} %all_gather.26, bf16[1,32,2048]{2,1,0:T(8,128)(2,1)S(1)} %copy-done.2), kind=kOutput, calls=%fused_computation.18 | convolution fusion | flops 243269632 | bytes 15454208 | tf_op jit(solution)/shard_map/dot_general | solution.py:45
  221.0 5.5 %all_gather.31 = bf16[32,1856]{1,0:T(8,128)(2,1)S(1)} all-gather(bf16[8,1856]{1,0:T(8,128)(2,1)S(1)} %get-tuple-element.14), channel_id=1, replica_groups=mesh['seq'=8,'tp'=4] {'tp'}, dimensions={0}, use_global_device_ids=true | all-gather | bytes 148480 | tf_op jit(solution)/shard_map/all_gather | solution.py:40
  226.5 5.4 %all_gather.27 = bf16[32,1856]{1,0:T(8,128)(2,1)S(1)} all-gather(bf16[8,1856]{1,0:T(8,128)(2,1)S(1)} %get-tuple-element.12), channel_id=1, replica_groups=mesh['seq'=8,'tp'=4] {'tp'}, dimensions={0}, use_global_device_ids=true | all-gather | bytes 148480 | tf_op jit(solution)/shard_map/all_gather | solution.py:40
  231.9 5.6 %all_gather.30 = bf16[32,1856]{1,0:T(8,128)(2,1)S(1)} all-gather(bf16[8,1856]{1,0:T(8,128)(2,1)S(1)} %get-tuple-element.15), channel_id=1, replica_groups=mesh['seq'=8,'tp'=4] {'tp'}, dimensions={0}, use_global_device_ids=true | all-gather | bytes 148480 | tf_op jit(solution)/shard_map/all_gather | solution.py:39
  237.5 7.8 %fusion.9 = f32[1856,2048]{1,0:T(8,128)} fusion(bf16[32,1856]{1,0:T(8,128)(2,1)S(1)} %all_gather.27, bf16[1,32,2048]{2,1,0:T(8,128)(2,1)S(1)} %copy-done.2), kind=kOutput, calls=%fused_computation.16 | convolution fusion | flops 243269632 | bytes 15454208 | tf_op jit(solution)/shard_map/dot_general | solution.py:48
  245.3 2.1 convolution_add_fusion.2
  248.9 1.4 convolution_add_fusion.1
  250.3 7.8 %convolution_add_fusion = f32[1856,2048]{1,0:T(8,128)} fusion(f32[1856,2048]{1,0:T(8,128)S(1)} %fusion.17, f32[32,1856]{1,0:T(8,128)S(1)} %copy-done.6, f32[32,1856]{1,0:T(8,128)S(1)} %copy-done.7, bf16[1,32,2048]{2,0,1:T(2,128)(2,1)S(1)} %copy-done.4), kind=kOutput, calls=%fused_computation.2 | convolution fusion | flops 247427072 | bytes 31014912 | tf_op jit(solution)/shard_map/dot_general | solution.py:42
  258.2 13.1 %add_bitcast_fusion = f32[2048,1856]{0,1:T(8,128)} fusion(f32[1856,2048]{1,0:T(8,128)} %fusion.9, bf16[32,1856]{1,0:T(8,128)(2,1)S(1)} %all_gather.31, bf16[1,32,2048]{2,1,0:T(8,128)(2,1)S(1)} %copy.20), kind=kOutput, calls=%fused_computation | convolution fusion | flops 247070720 | bytes 30658560 | tf_op jit(solution)/shard_map/dot_general | solution.py:48
  271.3 13.2 %add_bitcast_fusion.1 = f32[2048,1856]{0,1:T(8,128)} fusion(f32[1856,2048]{1,0:T(8,128)} %fusion.11, bf16[32,1856]{1,0:T(8,128)(2,1)S(1)} %all_gather.30, bf16[1,32,2048]{2,1,0:T(8,128)(2,1)S(1)} %copy.20), kind=kOutput, calls=%fused_computation.1 | convolution fusion | flops 247070720 | bytes 30658560 | tf_op jit(solution)/shard_map/dot_general | solution.py:45
  284.5 43.3 %all-reduce.10 = (bf16[32,2048]{1,0:T(8,128)(2,1)S(1)}, bf16[32,2048]{1,0:T(8,128)(2,1)S(1)}) all-reduce(f32[32,2048]{1,0:T(8,128)S(1)} %convolution_add_fusion.1, f32[32,2048]{1,0:T(8,128)S(1)} %copy-done.5), channel_id=9, replica_groups=mesh['seq'=8,'tp'=4] {'seq'}, use_global_device_ids=true, to_apply=%region_7.8.clone | all-reduce | flops 131072 | bytes 786432
  (60 shorter events, 7.8 us)
Async XLA Ops:
  7.2 193.8 %all-reduce.9.cloned.1.call-start = ((), (), s32[]{:S(2)}) async-start(), calls=%async_computation | async-start | bytes 2949120 | tf_op jit(solution)/shard_map/psum | solution.py:23
  7.2 71.1 %copy-start = (bf16[2048,1856]{0,1:T(8,128)(2,1)S(1)}, bf16[2048,1856]{0,1:T(8,128)(2,1)}, u32[]{:S(2)}) copy-start(bf16[2048,1856]{0,1:T(8,128)(2,1)} %param.8) | copy-start | bytes 22806532
  71.9 6.4 %copy-start.1 = (bf16[1,32,2048]{2,1,0:T(8,128)(2,1)}, bf16[1,32,2048]{2,1,0:T(8,128)(2,1)S(1)}, u32[]{:S(2)}) copy-start(bf16[1,32,2048]{2,1,0:T(8,128)(2,1)S(1)} %copy.18) | copy-start | bytes 393220
  71.9 9.4 %slice-start = ((s8[7602176]{0:T(1024)(128)(4,1)}), s8[4194304]{0:T(1024)(128)(4,1)S(1)}, s32[]{:S(2)}) async-start(s8[7602176]{0:T(1024)(128)(4,1)} %bitcast.56), calls=%async_computation.1 | async-start | bytes 8388608
  78.3 3.0 slice-start.1
  81.3 6.1 %copy-start.8 = (bf16[2,4,2048]{2,1,0:T(4,128)(2,1)S(1)}, bf16[2,4,2048]{2,1,0:T(4,128)(2,1)}, u32[]{:S(2)}) copy-start(bf16[2,4,2048]{2,1,0:T(4,128)(2,1)} %param.6) | copy-start | bytes 98308
  81.3 69.8 %slice-start.6 = ((s8[7602176]{0:T(1024)(128)(4,1)}), s8[4194304]{0:T(1024)(128)(4,1)S(1)}, s32[]{:S(2)}) async-start(s8[7602176]{0:T(1024)(128)(4,1)} %bitcast.62), calls=%async_computation.7 | async-start | bytes 8388608
  84.4 66.8 %slice-start.7 = ((s8[7602176]{0:T(1024)(128)(4,1)}), s8[3407872]{0:T(1024)(128)(4,1)S(1)}, s32[]{:S(2)}) async-start(s8[7602176]{0:T(1024)(128)(4,1)} %bitcast.62), calls=%async_computation.8 | async-start | bytes 6815744
  118.3 37.0 %copy-start.3 = (bf16[1,32,2048]{2,0,1:T(2,128)(2,1)}, bf16[1,32,2048]{2,0,1:T(2,128)(2,1)S(1)}, u32[]{:S(2)}) copy-start(bf16[1,32,2048]{2,0,1:T(2,128)(2,1)S(1)} %all-gather.2) | copy-start | bytes 393220
  151.2 7.1 %copy-start.10 = (u32[32]{0:T(128)S(1)}, u32[32]{0:T(128)}, u32[]{:S(2)}) copy-start(u32[32]{0:T(128)} %constant.23) | copy-start | bytes 388
  151.2 7.8 %copy-start.9 = (u32[32]{0:T(128)S(1)}, u32[32]{0:T(128)}, u32[]{:S(2)}) copy-start(u32[32]{0:T(128)} %constant.19) | copy-start | bytes 388
  158.3 52.6 %slice-start.2 = ((s8[7602176]{0:T(1024)(128)(4,1)}), s8[3407872]{0:T(1024)(128)(4,1)S(1)}, s32[]{:S(2)}) async-start(s8[7602176]{0:T(1024)(128)(4,1)} %bitcast.58), calls=%async_computation.3 | async-start | bytes 6815744
  201.0 9.9 %slice-start.3 = ((s8[7602176]{0:T(1024)(128)(4,1)}), s8[4194304]{0:T(1024)(128)(4,1)S(1)}, s32[]{:S(2)}) async-start(s8[7602176]{0:T(1024)(128)(4,1)} %bitcast.58), calls=%async_computation.4 | async-start | bytes 8388608
  210.9 1.4 copy-start.2
  212.3 7.8 %copy-start.6 = (f32[32,1856]{1,0:T(8,128)S(1)}, f32[32,1856]{1,0:T(8,128)}, u32[]{:S(2)}) copy-start(f32[32,1856]{1,0:T(8,128)} %get-tuple-element.6) | copy-start | bytes 712708
  212.3 7.8 %copy-start.7 = (f32[32,1856]{1,0:T(8,128)S(1)}, f32[32,1856]{1,0:T(8,128)}, u32[]{:S(2)}) copy-start(f32[32,1856]{1,0:T(8,128)} %get-tuple-element.8) | copy-start | bytes 712708
  212.3 33.0 %slice-start.4 = ((s8[7602176]{0:T(1024)(128)(4,1)}), s8[4194304]{0:T(1024)(128)(4,1)S(1)}, s32[]{:S(2)}) async-start(s8[7602176]{0:T(1024)(128)(4,1)} %bitcast.60), calls=%async_computation.5 | async-start | bytes 8388608
  221.0 24.3 %slice-start.5 = ((s8[7602176]{0:T(1024)(128)(4,1)}), s8[3407872]{0:T(1024)(128)(4,1)S(1)}, s32[]{:S(2)}) async-start(s8[7602176]{0:T(1024)(128)(4,1)} %bitcast.60), calls=%async_computation.6 | async-start | bytes 6815744
  248.9 1.5 copy-start.4
  271.3 13.2 %copy-start.5 = (f32[32,2048]{1,0:T(8,128)S(1)}, f32[32,2048]{1,0:T(8,128)}, u32[]{:S(2)}) copy-start(f32[32,2048]{1,0:T(8,128)} %convolution_add_fusion.2) | copy-start | bytes 786436
Sparse Core Ops, SparseCore 0:
  158.4 42.5 all-reduce.8
where the time goes:
time: 336 us; the launch traced here: 335 us
  blocking collectives  192 us (57%)
  matrix products  82.2 us (24%)
  waiting for transfers between devices  40.2 us (12%)
  between operations  15.5 us (5%)
    all_gather x2, blocking collectives, per_device(): whole_grad = lax.all_gather(out_grad[index], 'seq', axis=0, tiled=True)  63.7 us
    all_gather x2, blocking collectives, per_device(): whole_in = lax.all_gather(inputs[index], 'seq', axis=0, tiled=True)  63.6 us
    unnamed x1, blocking collectives  43.3 us
    psum x1, waiting for transfers between devices, per_device(): gate, up_proj = lax.psum((gate_part, up_part), 'tp')  40.2 us
    dot_general x2, matrix products, per_device(): lax.dot_general(whole_in, front_unit_gate, contract_first, preferred_elem...  21 us
    dot_general x2, matrix products, per_device(): lax.dot_general(whole_in, front_unit_up, contract_first, preferred_elemen...  20.9 us
    dot_general x2, matrix products, per_device(): lax.dot_general(hidden, whole_grad, contract_first, preferred_element_typ...  11.4 us
    all_gather x2, blocking collectives, per_device(): front_unit_gate = lax.all_gather(gate_local, 'tp', axis=0, tiled=True)  11 us
  transfers between devices with their start and end apart: 1, of which 1 were waited for; matrix products, arithmetic and copies ran while one was open for 0% of the time, Pallas kernels for 0%

commit v1 on v0

v1 whole, which is shorter than its diff:
```python
import jax
import jax.numpy as jnp
from jax import lax
from jax.sharding import PartitionSpec as P

CONTRACT_FIRST = (((0,), (0,)), ((), ()))
CONTRACT_LAST = (((1,), (1,)), ((), ()))


def swap(value, axis, bit):
    count = lax.axis_size(axis)
    return lax.ppermute(value, axis, [(index, index ^ bit) for index in range(count)])


def bits_of(count):
    return [1 << power for power in reversed(range(count.bit_length() - 1))]


def dot(left, right, dims):
    return lax.dot_general(left, right, dims, preferred_element_type=jnp.float32)


def per_device(inputs, out_grad, gate_weight, up_weight, down_weight):
    blocks, local_rows, width = inputs.shape
    seq_bits = bits_of(lax.axis_size("seq"))
    tp_bits = bits_of(lax.axis_size("tp"))
    odd = (lax.axis_index("tp") & 1) == 1

    def gather(value):
        value = value.reshape(blocks * local_rows, width)
        for bit in seq_bits[:-1]:
            value = jnp.concatenate([value, swap(value, "seq", bit)])
        other = swap(value, "seq", seq_bits[-1])
        return jnp.concatenate([jnp.where(odd, other, value), jnp.where(odd, value, other)])

    def reduce(part):
        half = part.shape[0] // 2
        total = part[:half] + swap(part[half:], "tp", 1)
        for bit in tp_bits[:-1]:
            total = total + swap(total.astype(jnp.bfloat16), "tp", bit).astype(jnp.float32)
        return total

    def spread(value):
        return jnp.concatenate([value, swap(value, "tp", 1)])

    whole_in = gather(inputs)
    whole_grad = gather(out_grad)
    gate = reduce(jnp.dot(whole_in, gate_weight, preferred_element_type=jnp.float32))
    up_proj = reduce(jnp.dot(whole_in, up_weight, preferred_element_type=jnp.float32))
    hidden_grad = reduce(dot(whole_grad, down_weight, CONTRACT_LAST))
    sig = jax.nn.sigmoid(gate)
    hidden = spread((gate * sig * up_proj).astype(jnp.bfloat16))
    up_unit = spread((hidden_grad * gate * sig).astype(jnp.bfloat16))
    gate_unit = spread(
        (hidden_grad * up_proj * sig * (1.0 + gate * (1.0 - sig))).astype(jnp.bfloat16)
    )
    back = dot(gate_unit, gate_weight, CONTRACT_LAST) + dot(up_unit, up_weight, CONTRACT_LAST)
    half = back.shape[0] // 2
    sent = jnp.where(odd, back[:half], back[half:])
    kept = jnp.where(odd, back[half:], back[:half])
    back = kept + swap(sent, "seq", seq_bits[-1])
    for bit in reversed(seq_bits[:-1]):
        half = back.shape[0] // 2
        back = back[:half] + swap(back[half:], "seq", bit)
    input_grad = back.astype(jnp.bfloat16).reshape(blocks, local_rows, width)
    down_grad = dot(hidden, whole_grad, CONTRACT_FIRST)
    gate_grad = dot(whole_in, gate_unit, CONTRACT_FIRST)
    up_grad = dot(whole_in, up_unit, CONTRACT_FIRST)
    return input_grad, gate_grad, up_grad, down_grad


def solution(mesh):
    return jax.shard_map(
        per_device,
        mesh=mesh,
        in_specs=(
            P(None, "seq", "tp"),
            P(None, "seq", "tp"),
            P("tp", "seq"),
            P("tp", "seq"),
            P("seq", "tp"),
        ),
        out_specs=(P(None, "seq", "tp"), P("tp", "seq"), P("tp", "seq"), P("seq", "tp")),
        check_vma=False,
    )
```

time: 336 us -> 75.1 us (0.22)
  blocking collectives: 192 us -> 0 us
  matrix products: 82.2 us -> 36.9 us
  waiting for transfers between devices: 40.2 us -> 13.3 us
  starting transfers between devices: 0.04 us -> 21.1 us
  between operations: 15.5 us -> 0.87 us
    all_gather x8 -> x0, blocking collectives: 149 us -> none  [the longest x2 63.7 us: per_device(): whole_grad = lax.all_gather(out_grad[index], 'seq', axis=0, tiled=True)]
    unnamed x1 -> x0, blocking collectives: 43.3 us -> none
    psum x1 -> x0, waiting for transfers between devices: 40.2 us -> none  [per_device(): gate, up_proj = lax.psum((gate_part, up_part), 'tp')]
    dot_general x14 -> x7, matrix products: 72.8 us -> 34.5 us  [the longest x6 32.1 us: dot(): lax.dot_general(left, right, dims, preferred_element_type=jnp.float32)]
    ppermute x0 -> x18, starting transfers between devices: none -> 21.1 us  [swap(): lax.ppermute(value, axis, [(index, index ^ bit) for index in range(count)])]
    ppermute x0 -> x18, waiting for transfers between devices: none -> 13.3 us  [swap(): lax.ppermute(value, axis, [(index, index ^ bit) for index in range(count)])]
    dot_general x2 -> x1, matrix products: 9.39 us -> 2.38 us  [per_device(): jnp.dot(whole_in, gate_weight, preferred_element_type=jnp.float32)]
  transfers between devices with their start and end apart: 1 -> 18, of which waited for: 1 -> 8; matrix products, arithmetic and copies ran while one was open for 0% -> 51% of each run, Pallas kernels for 0% -> 0%
where the time goes in v1:
time: 75.1 us; the launch traced here: 74.9 us
  matrix products  36.9 us (49%)
  starting transfers between devices  21.1 us (28%)
  waiting for transfers between devices  13.3 us (18%)
  local copies, waits for them, and re-layouts  2.3 us (3%)
  between operations  0.87 us (1%)
    dot_general x6, matrix products, dot(): lax.dot_general(left, right, dims, preferred_element_type=jnp.float32)  32.1 us
    ppermute x18, starting transfers between devices, swap(): lax.ppermute(value, axis, [(index, index ^ bit) for index in range(count)])  21.1 us
    ppermute x18, waiting for transfers between devices, swap(): lax.ppermute(value, axis, [(index, index ^ bit) for index in range(count)])  13.3 us
    dot_general x1, matrix products, per_device(): jnp.dot(whole_in, up_weight, preferred_element_type=jnp.float32)  2.38 us
    dot_general x1, matrix products, per_device(): jnp.dot(whole_in, gate_weight, preferred_element_type=jnp.float32)  2.38 us
    reshape x2, local copies, waits for them, and re-layouts, gather(): value = value.reshape(blocks * local_rows, width)  1.54 us
  transfers between devices with their start and end apart: 18, of which 8 were waited for; matrix products, arithmetic and copies ran while one was open for 51% of the time, Pallas kernels for 0%

profile of v1, /device:TPU:0, one launch (start us, length us, event | category | flops | bytes accessed | tf_op | source)
XLA Modules:
  0.0 74.9 jit_solution(1637178095513839929)
XLA Ops:
  1.4 4.1 %collective-permute-start = (bf16[8,2048]{1,0:T(8,128)(2,1)S(1)}, bf16[8,2048]{1,0:T(8,128)(2,1)S(1)}, u32[]{:S(2)}, u32[]{:S(2)}) collective-permute-start(bf16[8,2048]{1,0:T(8,128)(2,1)S(1)} %reshape.17), channel_id=1, source_target_pairs={{0,16},{4,20},{8,24},{12,28},{16,0},{20,4},{24,8},{28,12},{1,17},{... | collective-permute-start | bytes 98312 | tf_op jit(solution)/shard_map/ppermute | solution.py:12
  6.4 1.4 %collective-permute-done = bf16[8,2048]{1,0:T(8,128)(2,1)S(1)} collective-permute-done((bf16[8,2048]{1,0:T(8,128)(2,1)S(1)}, bf16[8,2048]{1,0:T(8,128)(2,1)S(1)}, u32[]{:S(2)}, u32[]{:S(2)}) %collective-permute-start) | collective-permute-done | bytes 32800 | tf_op jit(solution)/shard_map/ppermute | solution.py:12
  7.8 1.8 %collective-permute-start.1 = (bf16[16,2048]{1,0:T(8,128)(2,1)S(1)}, bf16[16,2048]{1,0:T(8,128)(2,1)S(1)}, u32[]{:S(2)}, u32[]{:S(2)}) collective-permute-start(bf16[16,2048]{1,0:T(8,128)(2,1)S(1)} %pad_maximum_fusion.10), channel_id=1, source_target_pairs={{0,8},{4,12},{8,0},{12,4},{16,24},{20,28},{24,16},{28,20},{1,9},{5... | collective-permute-start | bytes 196616 | tf_op jit(solution)/shard_map/ppermute | solution.py:12
  9.6 1.6 %collective-permute-done.5 = bf16[8,2048]{1,0:T(8,128)(2,1)S(1)} collective-permute-done((bf16[8,2048]{1,0:T(8,128)(2,1)S(1)}, bf16[8,2048]{1,0:T(8,128)(2,1)S(1)}, u32[]{:S(2)}, u32[]{:S(2)}) %collective-permute-start.5) | collective-permute-done | bytes 32800 | tf_op jit(solution)/shard_map/ppermute | solution.py:12
  11.2 1.6 %collective-permute-start.6 = (bf16[16,2048]{1,0:T(8,128)(2,1)S(1)}, bf16[16,2048]{1,0:T(8,128)(2,1)S(1)}, u32[]{:S(2)}, u32[]{:S(2)}) collective-permute-start(bf16[16,2048]{1,0:T(8,128)(2,1)S(1)} %pad_maximum_fusion.11), channel_id=1, source_target_pairs={{0,8},{4,12},{8,0},{12,4},{16,24},{20,28},{24,16},{28,20},{1,9},{5... | collective-permute-start | bytes 196616 | tf_op jit(solution)/shard_map/ppermute | solution.py:12
  12.8 1.6 %collective-permute-start.2 = (bf16[32,2048]{1,0:T(8,128)(2,1)S(1)}, bf16[32,2048]{1,0:T(8,128)(2,1)S(1)}, u32[]{:S(2)}, u32[]{:S(2)}) collective-permute-start(bf16[32,2048]{1,0:T(8,128)(2,1)S(1)} %constant_dynamic-update-slice_fusion), channel_id=1, source_target_pairs={{0,4},{4,0},{8,12},{12,8},{16,20},{20,16},{24,28},{28,24},{1,5},{5... | collective-permute-start | bytes 393224 | tf_op jit(solution)/shard_map/ppermute | solution.py:12
  15.5 1.5 %collective-permute-start.7 = (bf16[32,2048]{1,0:T(8,128)(2,1)S(1)}, bf16[32,2048]{1,0:T(8,128)(2,1)S(1)}, u32[]{:S(2)}, u32[]{:S(2)}) collective-permute-start(bf16[32,2048]{1,0:T(8,128)(2,1)S(1)} %constant_dynamic-update-slice_fusion.3), channel_id=1, source_target_pairs={{0,4},{4,0},{8,12},{12,8},{16,20},{20,16},{24,28},{28,24},{1,5},{5... | collective-permute-start | bytes 393224 | tf_op jit(solution)/shard_map/ppermute | solution.py:12
  17.0 1.2 %collective-permute-done.2 = bf16[32,2048]{1,0:T(8,128)(2,1)S(1)} collective-permute-done((bf16[32,2048]{1,0:T(8,128)(2,1)S(1)}, bf16[32,2048]{1,0:T(8,128)(2,1)S(1)}, u32[]{:S(2)}, u32[]{:S(2)}) %collective-permute-start.2) | collective-permute-done | bytes 131104 | tf_op jit(solution)/shard_map/ppermute | solution.py:12
  18.3 5.7 %fusion.4 = f32[64,1856]{1,0:T(8,128)S(1)} fusion(bf16[1856,2048]{1,0:T(8,128)(2,1)} %param.9, bf16[32,2048]{1,0:T(8,128)(2,1)S(1)} %get-tuple-element.12, bf16[32,2048]{1,0:T(8,128)(2,1)S(1)} %get-tuple-element.11), kind=kOutput, calls=%fused_computation.21 | convolution fusion | flops 487063552 | bytes 8339456 | tf_op jit(solution)/shard_map/dot_general | solution.py:20
  24.1 2.4 %fusion.16 = f32[64,1856]{1,0:T(8,128)S(1)} fusion(bf16[2048,1856]{0,1:T(8,128)(2,1)S(1)} %copy-done, bf16[32,2048]{1,0:T(8,128)(2,1)S(1)} %get-tuple-element.10, bf16[32,2048]{1,0:T(8,128)(2,1)S(1)} %get-tuple-element.9), kind=kOutput, calls=%fused_computation.47 | convolution fusion | flops 487063552 | bytes 8339456 | tf_op jit(solution)/shard_map/dot_general | solution.py:49
  27.1 2.4 %fusion.15 = f32[64,1856]{1,0:T(8,128)S(1)} fusion(bf16[2048,1856]{0,1:T(8,128)(2,1)S(1)} %bitcast.6, bf16[32,2048]{1,0:T(8,128)(2,1)S(1)} %get-tuple-element.10, bf16[32,2048]{1,0:T(8,128)(2,1)S(1)} %get-tuple-element.9), kind=kOutput, calls=%fused_computation.46 | convolution fusion | flops 487063552 | bytes 8339456 | tf_op jit(solution)/shard_map/dot_general | solution.py:48
  29.6 1.6 %collective-permute-start.4 = (bf16[32,1856]{1,0:T(8,128)(2,1)S(1)}, bf16[32,1856]{1,0:T(8,128)(2,1)S(1)}, u32[]{:S(2)}, u32[]{:S(2)}) collective-permute-start(bf16[32,1856]{1,0:T(8,128)(2,1)S(1)} %fusion.17), channel_id=1, source_target_pairs={{0,2},{1,3},{2,0},{3,1},{4,6},{5,7},{6,4},{7,5},{8,10},{9,11},{10,... | collective-permute-start | bytes 356360 | tf_op jit(solution)/shard_map/ppermute | solution.py:12
  31.9 1.6 %collective-permute-start.11 = (bf16[32,1856]{1,0:T(8,128)(2,1)S(1)}, bf16[32,1856]{1,0:T(8,128)(2,1)S(1)}, u32[]{:S(2)}, u32[]{:S(2)}) collective-permute-start(bf16[32,1856]{1,0:T(8,128)(2,1)S(1)} %get-tuple-element.4), channel_id=1, source_target_pairs={{0,2},{1,3},{2,0},{3,1},{4,6},{5,7},{6,4},{7,5},{8,10},{9,11},{10,... | collective-permute-start | bytes 356360 | tf_op jit(solution)/shard_map/ppermute | solution.py:12
  33.4 2.5 %collective-permute-done.4 = bf16[32,1856]{1,0:T(8,128)(2,1)S(1)} collective-permute-done((bf16[32,1856]{1,0:T(8,128)(2,1)S(1)}, bf16[32,1856]{1,0:T(8,128)(2,1)S(1)}, u32[]{:S(2)}, u32[]{:S(2)}) %collective-permute-start.4) | collective-permute-done | bytes 118816 | tf_op jit(solution)/shard_map/ppermute | solution.py:12
  35.9 2.6 %collective-permute-done.9 = bf16[32,1856]{1,0:T(8,128)(2,1)S(1)} collective-permute-done((bf16[32,1856]{1,0:T(8,128)(2,1)S(1)}, bf16[32,1856]{1,0:T(8,128)(2,1)S(1)}, u32[]{:S(2)}, u32[]{:S(2)}) %collective-permute-start.9) | collective-permute-done | bytes 118816 | tf_op jit(solution)/shard_map/ppermute | solution.py:12
  38.5 2.1 %collective-permute-done.11 = bf16[32,1856]{1,0:T(8,128)(2,1)S(1)} collective-permute-done((bf16[32,1856]{1,0:T(8,128)(2,1)S(1)}, bf16[32,1856]{1,0:T(8,128)(2,1)S(1)}, u32[]{:S(2)}, u32[]{:S(2)}) %collective-permute-start.11) | collective-permute-done | bytes 118816 | tf_op jit(solution)/shard_map/ppermute | solution.py:12
  42.3 1.5 %fusion.6 = f32[64,2048]{1,0:T(8,128)S(1)} fusion(bf16[2048,1856]{0,1:T(8,128)(2,1)S(1)} %copy-done, bf16[32,1856]{1,0:T(8,128)(2,1)S(1)} %collective-permute-done.13, bf16[32,1856]{1,0:T(8,128)(2,1)S(1)} %get-tuple-element.8), kind=kOutput, calls=%fused_computation.23 | convolution fusion | flops 487014400 | bytes 8364032 | tf_op jit(solution)/shard_map/dot_general | solution.py:20
  43.8 1.5 %convolution_add_fusion = f32[64,2048]{1,0:T(8,128)S(1)} fusion(f32[64,2048]{1,0:T(8,128)S(1)} %fusion.6, bf16[2048,1856]{0,1:T(8,128)(2,1)S(1)} %bitcast.6, bf16[32,1856]{1,0:T(8,128)(2,1)S(1)} %collective-permute-done.12, bf16[32,1856]{1,0:T(8,128)(2,1)S(1)} %get-tuple-element.7), kind=kOutput, calls=%fused_computation | convolution fusion | flops 487145472 | bytes 8888320 | tf_op jit(solution)/shard_map/dot_general | solution.py:20
  45.3 1.6 %collective-permute-start.14 = (f32[32,2048]{1,0:T(8,128)S(1)}, f32[32,2048]{1,0:T(8,128)S(1)}, u32[]{:S(2)}, u32[]{:S(2)}) collective-permute-start(f32[32,2048]{1,0:T(8,128)S(1)} %slice_select_fusion), channel_id=1, source_target_pairs={{0,4},{4,0},{8,12},{12,8},{16,20},{20,16},{24,28},{28,24},{1,5},{5... | collective-permute-start | bytes 786440 | tf_op jit(solution)/shard_map/ppermute | solution.py:12
  46.9 7.8 %fusion.7 = f32[2048,1856]{0,1:T(8,128)} fusion(bf16[32,1856]{1,0:T(8,128)(2,1)S(1)} %collective-permute-done.12, bf16[32,1856]{1,0:T(8,128)(2,1)S(1)} %get-tuple-element.7, bf16[32,2048]{1,0:T(8,128)(2,1)S(1)} %get-tuple-element.10, bf16[32,2048]{1,0:T(8,128)(2,1)S(1)} %get-tuple-element.9), kind=kOutput, calls=%fused_computation.24 | convolution fusion | flops 487538688 | bytes 15704064 | tf_op jit(solution)/shard_map/dot_general | solution.py:20
  54.8 1.5 %collective-permute-start.15 = (f32[16,2048]{1,0:T(8,128)S(1)}, f32[16,2048]{1,0:T(8,128)S(1)}, u32[]{:S(2)}, u32[]{:S(2)}) collective-permute-start(f32[16,2048]{1,0:T(8,128)S(1)} %slice.59), channel_id=1, source_target_pairs={{0,8},{4,12},{8,0},{12,4},{16,24},{20,28},{24,16},{28,20},{1,9},{5... | collective-permute-start | bytes 393224 | tf_op jit(solution)/shard_map/ppermute | solution.py:12
  56.3 7.8 %fusion.5 = f32[2048,1856]{0,1:T(8,128)} fusion(bf16[32,1856]{1,0:T(8,128)(2,1)S(1)} %collective-permute-done.13, bf16[32,1856]{1,0:T(8,128)(2,1)S(1)} %get-tuple-element.8, bf16[32,2048]{1,0:T(8,128)(2,1)S(1)} %get-tuple-element.10, bf16[32,2048]{1,0:T(8,128)(2,1)S(1)} %get-tuple-element.9), kind=kOutput, calls=%fused_computation.22 | convolution fusion | flops 487538688 | bytes 15704064 | tf_op jit(solution)/shard_map/dot_general | solution.py:20
  64.2 2.2 %collective-permute-start.16 = (f32[8,2048]{1,0:T(8,128)S(1)}, f32[8,2048]{1,0:T(8,128)S(1)}, u32[]{:S(2)}, u32[]{:S(2)}) collective-permute-start(f32[8,2048]{1,0:T(8,128)S(1)} %slice.61), channel_id=1, source_target_pairs={{0,16},{4,20},{8,24},{12,28},{16,0},{20,4},{24,8},{28,12},{1,17},{... | collective-permute-start | bytes 196616 | tf_op jit(solution)/shard_map/ppermute | solution.py:12
  66.4 7.8 %fusion = f32[1856,2048]{1,0:T(8,128)} fusion(bf16[32,1856]{1,0:T(8,128)(2,1)S(1)} %collective-permute-done.17, bf16[32,1856]{1,0:T(8,128)(2,1)S(1)} %get-tuple-element.6, bf16[32,2048]{1,0:T(8,128)(2,1)S(1)} %get-tuple-element.12, bf16[32,2048]{1,0:T(8,128)(2,1)S(1)} %get-tuple-element.11), kind=kOutput, calls=%fused_computation.10 | convolution fusion | flops 487538688 | bytes 15704064 | tf_op jit(solution)/shard_map/dot_general | solution.py:20
  (53 shorter events, 6.6 us)
Async XLA Ops:
  1.4 6.4 %collective-permute-start = (bf16[8,2048]{1,0:T(8,128)(2,1)S(1)}, bf16[8,2048]{1,0:T(8,128)(2,1)S(1)}, u32[]{:S(2)}, u32[]{:S(2)}) collective-permute-start(bf16[8,2048]{1,0:T(8,128)(2,1)S(1)} %reshape.17), channel_id=1, source_target_pairs={{0,16},{4,20},{8,24},{12,28},{16,0},{20,4},{24,8},{28,12},{1,17},{... | collective-permute-start | bytes 98312 | tf_op jit(solution)/shard_map/ppermute | solution.py:12
  6.3 4.9 %collective-permute-start.5 = (bf16[8,2048]{1,0:T(8,128)(2,1)S(1)}, bf16[8,2048]{1,0:T(8,128)(2,1)S(1)}, u32[]{:S(2)}, u32[]{:S(2)}) collective-permute-start(bf16[8,2048]{1,0:T(8,128)(2,1)S(1)} %reshape.18), channel_id=1, source_target_pairs={{0,16},{4,20},{8,24},{12,28},{16,0},{20,4},{24,8},{28,12},{1,17},{... | collective-permute-start | bytes 98312 | tf_op jit(solution)/shard_map/ppermute | solution.py:12
  6.4 17.7 %copy-start = (bf16[2048,1856]{0,1:T(8,128)(2,1)S(1)}, bf16[2048,1856]{0,1:T(8,128)(2,1)}, u32[]{:S(2)}) copy-start(bf16[2048,1856]{0,1:T(8,128)(2,1)} %param.8) | copy-start | bytes 22806532
  7.8 5.0 %collective-permute-start.1 = (bf16[16,2048]{1,0:T(8,128)(2,1)S(1)}, bf16[16,2048]{1,0:T(8,128)(2,1)S(1)}, u32[]{:S(2)}, u32[]{:S(2)}) collective-permute-start(bf16[16,2048]{1,0:T(8,128)(2,1)S(1)} %pad_maximum_fusion.10), channel_id=1, source_target_pairs={{0,8},{4,12},{8,0},{12,4},{16,24},{20,28},{24,16},{28,20},{1,9},{5... | collective-permute-start | bytes 196616 | tf_op jit(solution)/shard_map/ppermute | solution.py:12
  11.2 4.3 %collective-permute-start.6 = (bf16[16,2048]{1,0:T(8,128)(2,1)S(1)}, bf16[16,2048]{1,0:T(8,128)(2,1)S(1)}, u32[]{:S(2)}, u32[]{:S(2)}) collective-permute-start(bf16[16,2048]{1,0:T(8,128)(2,1)S(1)} %pad_maximum_fusion.11), channel_id=1, source_target_pairs={{0,8},{4,12},{8,0},{12,4},{16,24},{20,28},{24,16},{28,20},{1,9},{5... | collective-permute-start | bytes 196616 | tf_op jit(solution)/shard_map/ppermute | solution.py:12
  12.8 5.4 %collective-permute-start.2 = (bf16[32,2048]{1,0:T(8,128)(2,1)S(1)}, bf16[32,2048]{1,0:T(8,128)(2,1)S(1)}, u32[]{:S(2)}, u32[]{:S(2)}) collective-permute-start(bf16[32,2048]{1,0:T(8,128)(2,1)S(1)} %constant_dynamic-update-slice_fusion), channel_id=1, source_target_pairs={{0,4},{4,0},{8,12},{12,8},{16,20},{20,16},{24,28},{28,24},{1,5},{5... | collective-permute-start | bytes 393224 | tf_op jit(solution)/shard_map/ppermute | solution.py:12
  15.5 8.6 %collective-permute-start.7 = (bf16[32,2048]{1,0:T(8,128)(2,1)S(1)}, bf16[32,2048]{1,0:T(8,128)(2,1)S(1)}, u32[]{:S(2)}, u32[]{:S(2)}) collective-permute-start(bf16[32,2048]{1,0:T(8,128)(2,1)S(1)} %constant_dynamic-update-slice_fusion.3), channel_id=1, source_target_pairs={{0,4},{4,0},{8,12},{12,8},{16,20},{20,16},{24,28},{28,24},{1,5},{5... | collective-permute-start | bytes 393224 | tf_op jit(solution)/shard_map/ppermute | solution.py:12
  18.2 8.8 %slice-start = ((s8[7602176]{0:T(1024)(128)(4,1)}), s8[4194304]{0:T(1024)(128)(4,1)S(1)}, s32[]{:S(2)}) async-start(s8[7602176]{0:T(1024)(128)(4,1)} %bitcast.5), calls=%async_computation | async-start | bytes 8388608
  24.0 3.1 %slice-start.1 = ((s8[7602176]{0:T(1024)(128)(4,1)}), s8[3407872]{0:T(1024)(128)(4,1)S(1)}, s32[]{:S(2)}) async-start(s8[7602176]{0:T(1024)(128)(4,1)} %bitcast.5), calls=%async_computation.1 | async-start | bytes 6815744
  24.0 5.6 %collective-permute-start.3 = (f32[32,1856]{1,0:T(8,128)S(1)}, f32[32,1856]{1,0:T(8,128)S(1)}, u32[]{:S(2)}, u32[]{:S(2)}) collective-permute-start(f32[32,1856]{1,0:T(8,128)S(1)} %slice.51), channel_id=1, source_target_pairs={{0,1},{1,0},{2,3},{3,2},{4,5},{5,4},{6,7},{7,6},{8,9},{9,8},{10,11... | collective-permute-start | bytes 712712 | tf_op jit(solution)/shard_map/ppermute | solution.py:12
  26.5 4.7 %collective-permute-start.8 = (f32[32,1856]{1,0:T(8,128)S(1)}, f32[32,1856]{1,0:T(8,128)S(1)}, u32[]{:S(2)}, u32[]{:S(2)}) collective-permute-start(f32[32,1856]{1,0:T(8,128)S(1)} %slice.53), channel_id=1, source_target_pairs={{0,1},{1,0},{2,3},{3,2},{4,5},{5,4},{6,7},{7,6},{8,9},{9,8},{10,11... | collective-permute-start | bytes 712712 | tf_op jit(solution)/shard_map/ppermute | solution.py:12
  29.5 2.3 %collective-permute-start.10 = (f32[32,1856]{1,0:T(8,128)S(1)}, f32[32,1856]{1,0:T(8,128)S(1)}, u32[]{:S(2)}, u32[]{:S(2)}) collective-permute-start(f32[32,1856]{1,0:T(8,128)S(1)} %slice.55), channel_id=1, source_target_pairs={{0,1},{1,0},{2,3},{3,2},{4,5},{5,4},{6,7},{7,6},{8,9},{9,8},{10,11... | collective-permute-start | bytes 712712 | tf_op jit(solution)/shard_map/ppermute | solution.py:12
  29.6 6.3 %collective-permute-start.4 = (bf16[32,1856]{1,0:T(8,128)(2,1)S(1)}, bf16[32,1856]{1,0:T(8,128)(2,1)S(1)}, u32[]{:S(2)}, u32[]{:S(2)}) collective-permute-start(bf16[32,1856]{1,0:T(8,128)(2,1)S(1)} %fusion.17), channel_id=1, source_target_pairs={{0,2},{1,3},{2,0},{3,1},{4,6},{5,7},{6,4},{7,5},{8,10},{9,11},{10,... | collective-permute-start | bytes 356360 | tf_op jit(solution)/shard_map/ppermute | solution.py:12
  31.2 7.3 %collective-permute-start.9 = (bf16[32,1856]{1,0:T(8,128)(2,1)S(1)}, bf16[32,1856]{1,0:T(8,128)(2,1)S(1)}, u32[]{:S(2)}, u32[]{:S(2)}) collective-permute-start(bf16[32,1856]{1,0:T(8,128)(2,1)S(1)} %fusion.18), channel_id=1, source_target_pairs={{0,2},{1,3},{2,0},{3,1},{4,6},{5,7},{6,4},{7,5},{8,10},{9,11},{10,... | collective-permute-start | bytes 356360 | tf_op jit(solution)/shard_map/ppermute | solution.py:12
  31.9 8.8 %collective-permute-start.11 = (bf16[32,1856]{1,0:T(8,128)(2,1)S(1)}, bf16[32,1856]{1,0:T(8,128)(2,1)S(1)}, u32[]{:S(2)}, u32[]{:S(2)}) collective-permute-start(bf16[32,1856]{1,0:T(8,128)(2,1)S(1)} %get-tuple-element.4), channel_id=1, source_target_pairs={{0,2},{1,3},{2,0},{3,1},{4,6},{5,7},{6,4},{7,5},{8,10},{9,11},{10,... | collective-permute-start | bytes 356360 | tf_op jit(solution)/shard_map/ppermute | solution.py:12
  40.9 1.4 %collective-permute-start.13 = (bf16[32,1856]{1,0:T(8,128)(2,1)S(1)}, bf16[32,1856]{1,0:T(8,128)(2,1)S(1)}, u32[]{:S(2)}, u32[]{:S(2)}) collective-permute-start(bf16[32,1856]{1,0:T(8,128)(2,1)S(1)} %get-tuple-element.8), channel_id=1, source_target_pairs={{0,1},{1,0},{2,3},{3,2},{4,5},{5,4},{6,7},{7,6},{8,9},{9,8},{10,11... | collective-permute-start | bytes 356360 | tf_op jit(solution)/shard_map/ppermute | solution.py:12
  41.0 25.4 %collective-permute-start.17 = (bf16[32,1856]{1,0:T(8,128)(2,1)S(1)}, bf16[32,1856]{1,0:T(8,128)(2,1)S(1)}, u32[]{:S(2)}, u32[]{:S(2)}) collective-permute-start(bf16[32,1856]{1,0:T(8,128)(2,1)S(1)} %get-tuple-element.6), channel_id=1, source_target_pairs={{0,1},{1,0},{2,3},{3,2},{4,5},{5,4},{6,7},{7,6},{8,9},{9,8},{10,11... | collective-permute-start | bytes 356360 | tf_op jit(solution)/shard_map/ppermute | solution.py:12
  41.5 2.3 %collective-permute-start.12 = (bf16[32,1856]{1,0:T(8,128)(2,1)S(1)}, bf16[32,1856]{1,0:T(8,128)(2,1)S(1)}, u32[]{:S(2)}, u32[]{:S(2)}) collective-permute-start(bf16[32,1856]{1,0:T(8,128)(2,1)S(1)} %get-tuple-element.7), channel_id=1, source_target_pairs={{0,1},{1,0},{2,3},{3,2},{4,5},{5,4},{6,7},{7,6},{8,9},{9,8},{10,11... | collective-permute-start | bytes 356360 | tf_op jit(solution)/shard_map/ppermute | solution.py:12
  45.3 9.4 %collective-permute-start.14 = (f32[32,2048]{1,0:T(8,128)S(1)}, f32[32,2048]{1,0:T(8,128)S(1)}, u32[]{:S(2)}, u32[]{:S(2)}) collective-permute-start(f32[32,2048]{1,0:T(8,128)S(1)} %slice_select_fusion), channel_id=1, source_target_pairs={{0,4},{4,0},{8,12},{12,8},{16,20},{20,16},{24,28},{28,24},{1,5},{5... | collective-permute-start | bytes 786440 | tf_op jit(solution)/shard_map/ppermute | solution.py:12
  54.8 9.3 %collective-permute-start.15 = (f32[16,2048]{1,0:T(8,128)S(1)}, f32[16,2048]{1,0:T(8,128)S(1)}, u32[]{:S(2)}, u32[]{:S(2)}) collective-permute-start(f32[16,2048]{1,0:T(8,128)S(1)} %slice.59), channel_id=1, source_target_pairs={{0,8},{4,12},{8,0},{12,4},{16,24},{20,28},{24,16},{28,20},{1,9},{5... | collective-permute-start | bytes 393224 | tf_op jit(solution)/shard_map/ppermute | solution.py:12
  64.2 10.1 %collective-permute-start.16 = (f32[8,2048]{1,0:T(8,128)S(1)}, f32[8,2048]{1,0:T(8,128)S(1)}, u32[]{:S(2)}, u32[]{:S(2)}) collective-permute-start(f32[8,2048]{1,0:T(8,128)S(1)} %slice.61), channel_id=1, source_target_pairs={{0,16},{4,20},{8,24},{12,28},{16,0},{20,4},{24,8},{28,12},{1,17},{... | collective-permute-start | bytes 196616 | tf_op jit(solution)/shard_map/ppermute | solution.py:12
